TPU v7x, 32 devices: a whole 2x2x4 slice. The times are simulated.
32 devices in a mesh: row: 4 (over z), col: 8 (over y, x, core).
Axes of the slice: x: 2, y: 2, z: 4, core: 2. Of those that a mesh axis runs over, the one named last changes fastest.
Arguments:
- adjacency: int32 [32768, 2048], P('col', 'row'), may hold values from -2147483648 to 2147483647, as said below
- frontier: bfloat16 [65536, 128], P(('row', 'col')), may hold values from 0 to 1, as said below
- visited: int32 [4, 32768], P(None, ('col', 'row')), may hold values from -2147483648 to 2147483647, as said below
Outputs:
- path_counts: float32 [32768, 128], P(('col', 'row'))
- reached_bits: int32 [4, 32768], P(None, ('col', 'row'))
Inputs may be any that keep to these rules, and one draw needn't show every extreme that they name: Bit k of adjacency[d, w] is the edge from source vertex 32 w + k to destination d; degrees and edge densities differ between vertices and between blocks of 128 by 128 vertices. `frontier`: values are zero or between 0.1 and 1. Bit k of visited[w, d] tells whether destination d was reached from root 32 w + k.
All inputs are finite; a program needn't handle non-finite values.
Results may differ from a plain program's by a relative error of at most 0.0003.
Values may be sent and summed in bfloat16 or wider, within the bound.
A program may use at most 64 MiB of HBM per device.

v0:
```python
import functools
import math

import jax
import jax.numpy as jnp
import numpy as np
from jax import lax
from jax.experimental import pallas as pl
from jax.experimental.pallas import tpu as pltpu
from jax.sharding import PartitionSpec as P

MESH = pl.DeviceIdType.MESH
LOW = 0.09
LEVELS = 65000.0


def expand_bits(words):
    one = jnp.full(words.shape, 1, jnp.float8_e4m3fn)
    zero = jnp.full(words.shape, 0, jnp.float8_e4m3fn)
    pieces = []
    for byte in range(4):
        part = (words >> (8 * byte)).astype(jnp.int8)
        for bit in range(8):
            mask = np.int8(-128) if bit == 7 else np.int8(1 << bit)
            pieces.append(jnp.where((part & mask) != 0, one, zero))
    return jnp.concatenate(pieces, axis=0)


def encode(value, scale):
    code = jnp.log(jnp.maximum(value, LOW)) * scale + (1.5 - math.log(LOW) * scale)
    code = jnp.where(value > 0, code, 0.0).astype(jnp.int32)
    return (code - 32768).astype(jnp.int16)


def decode(code, scale):
    code = code.astype(jnp.int32) + 32768
    value = jnp.exp((code - 1).astype(jnp.float32) * (1.0 / scale) + math.log(LOW))
    return jnp.where(code > 0, value, 0.0)


def flip(index, bit):
    return index + bit - 2 * bit * ((index // bit) % 2)


def kernel(
    n_row, n_col, adj, ft, visited, counts, bits,
    stage, words, fbuf, total, out_code, in_code,
    load_sem, own_sem, fsend, frecv, psend, precv,
):
    r, c = lax.axis_index("row"), lax.axis_index("col")
    dst, width = adj.shape
    depth = ft.shape[1]
    wide = width // n_col
    part = dst // n_row
    half = math.gcd(dst, 2048)
    halves = dst // half
    tile = stage.shape[1]
    tiles = dst // tile
    paired = n_col == 8
    scale = LEVELS / math.log(width * 32 * 1.01 / LOW)

    def load(t, slot):
        return pltpu.make_async_copy(
            adj.at[pl.ds(pl.multiple_of(t * tile, tile), tile), :], stage.at[slot], load_sem.at[slot]
        )

    load(0, 0).start()
    own = pltpu.make_async_copy(ft, fbuf.at[c], own_sem)
    own.start()

    if paired:
        mates = [flip(c, 1), flip(c, 2), flip(c, 4)]
    else:
        mates = [lax.rem(c + i, n_col) for i in range(1, n_col)]
    others = [lax.rem(r + i, n_row) for i in range(1, n_row)]
    barrier = pltpu.get_barrier_semaphore()
    for mate in mates:
        pl.semaphore_signal(barrier, inc=1, device_id={"col": mate}, device_id_type=MESH)
    for other in others:
        pl.semaphore_signal(barrier, inc=1, device_id={"row": other}, device_id_type=MESH)
    pl.semaphore_wait(barrier, len(mates) + len(others))

    def send(src, dst_ref, role, mate):
        return pltpu.make_async_remote_copy(
            src_ref=src, dst_ref=dst_ref, send_sem=fsend.at[role], recv_sem=frecv.at[role],
            device_id={"col": mate}, device_id_type=MESH,
        )

    if paired:
        pair, east, north = mates
        first, second = pl.ds(0, ft.shape[0] // 2), pl.ds(ft.shape[0] // 2, ft.shape[0] // 2)
        diagonal = flip(east, 4)
        slots = [pair, east, north, diagonal, diagonal, flip(pair, 2), flip(pair, 4), flip(diagonal, 1)]
        sends = [
            send(ft, fbuf.at[c], 0, pair),
            send(ft, fbuf.at[c], 1, east),
            send(ft, fbuf.at[c], 2, north),
            send(fbuf.at[east, first], fbuf.at[east, first], 3, north),
            send(fbuf.at[north, second], fbuf.at[north, second], 4, east),
            send(fbuf.at[east], fbuf.at[east], 5, pair),
            send(fbuf.at[north], fbuf.at[north], 6, pair),
            send(fbuf.at[diagonal], fbuf.at[diagonal], 7, pair),
        ]
        for role in (1, 2, 0):
            sends[role].start()

        def arrived(role):
            place = fbuf.at[slots[role]]
            if role == 3:
                place = fbuf.at[diagonal, first]
            if role == 4:
                place = fbuf.at[diagonal, second]
            send(place, place, role, pair).wait_recv()

    else:
        sends = [send(ft, fbuf.at[c], i, mate) for i, mate in enumerate(mates)]
        for copy in sends:
            copy.start()

    @pl.loop(0, tiles)
    def _(t):
        slot = lax.rem(t, 2)

        @pl.when(t + 1 < tiles)
        def _():
            load(t + 1, 1 - slot).start()

        load(t, slot).wait()
        words[:, pl.ds(pl.multiple_of(t * tile, tile), tile)] = stage[slot].T

    total[...] = jnp.zeros_like(total)
    own.wait()

    def product(slot, start, size):
        packed = words[pl.ds(pl.multiple_of(slot * wide, wide), wide), pl.ds(start, size)]
        return lax.dot_general(
            fbuf[slot], expand_bits(packed), (((1,), (0,)), ((), ())), preferred_element_type=jnp.float32
        )

    early = n_col - 2

    @pl.loop(0, early * halves)
    def _(t):
        step = t // halves
        start = pl.multiple_of(lax.rem(t, halves) * half, half)
        fresh = lax.rem(t, halves) == 0
        if paired:

            @pl.when(jnp.logical_and(fresh, step == 1))
            def _():
                arrived(0)

            @pl.when(jnp.logical_and(fresh, step == 2))
            def _():
                arrived(1)
                sends[3].start()
                sends[5].start()
                arrived(2)
                sends[4].start()
                sends[6].start()

            @pl.when(jnp.logical_and(fresh, step == 4))
            def _():
                arrived(5)

            @pl.when(jnp.logical_and(fresh, step == 5))
            def _():
                arrived(6)
                arrived(3)
                arrived(4)
                sends[7].start()

            slot = c
            for number, choice in enumerate((slots[0], slots[1], slots[2], slots[5], slots[6])):
                slot = jnp.where(step == number + 1, choice, slot)
        else:
            slot = lax.rem(c + n_col - step, n_col)

            @pl.when(jnp.logical_and(fresh, step > 0))
            def _():
                send(fbuf.at[slot], fbuf.at[slot], step - 1, mates[0]).wait_recv()

        total[:, pl.ds(start, half)] += product(slot, start, half)

    if paired:
        arrived(7)
        last = (slots[3], slots[7])
    else:
        last = (lax.rem(c + 2, n_col), lax.rem(c + 1, n_col))
        for slot, role in zip(last, (n_col - 3, n_col - 2)):
            send(fbuf.at[slot], fbuf.at[slot], role, mates[0]).wait_recv()

    def exchange(t, other):
        return pltpu.make_async_remote_copy(
            src_ref=out_code.at[t], dst_ref=in_code.at[t], send_sem=psend.at[t], recv_sem=precv.at[t],
            device_id={"row": other}, device_id_type=MESH,
        )

    @pl.loop(0, n_row)
    def _(t):
        other = lax.rem(r + 1 + t, n_row)
        start = pl.multiple_of(other * part, part)
        block = total[:, pl.ds(start, part)] + product(last[0], start, part)
        block = block + product(last[1], start, part)

        @pl.when(t < n_row - 1)
        def _():
            out_code[t] = encode(block, scale)
            exchange(t, other).start()

        @pl.when(t == n_row - 1)
        def _():
            total[:, pl.ds(0, part)] = block

    def received(t, value):
        exchange(t, others[0]).wait_recv()
        return value + decode(in_code[t], scale)

    reached = total[:, pl.ds(0, part)]
    for t in range(n_row - 1):
        reached = received(t, reached)
    place = lax.broadcasted_iota(jnp.int32, (32, part), 0)
    kept, added = [], []
    for word in range(visited.shape[0]):
        value = reached[word * 32 : word * 32 + 32]
        unseen = ((visited[word : word + 1, :] >> place) & 1) == 0
        kept.append(jnp.where(unseen, value, 0.0))
        marks = jnp.where(jnp.logical_and(unseen, value > 0), jnp.int32(1) << place, 0)
        added.append(jnp.sum(marks, axis=0, keepdims=True))
    counts[...] = jnp.concatenate(kept, axis=0).T
    bits[...] = visited[...] | jnp.concatenate(added, axis=0)
    for copy in sends:
        copy.wait_send()
    for t in range(n_row - 1):
        exchange(t, others[0]).wait_send()


ROLES = 19


def unpack(packed):
    one = jnp.full((32, packed.shape[1]), 1, jnp.float8_e4m3fn)
    zero = jnp.full((32, packed.shape[1]), 0, jnp.float8_e4m3fn)
    pieces = []
    for block in range(packed.shape[0] // 32):
        part = packed[block * 32 : block * 32 + 32]
        for bit in range(8):
            mask = np.int8(-128) if bit == 7 else np.int8(1 << bit)
            pieces.append(jnp.where((part & mask) != 0, one, zero))
    return jnp.concatenate(pieces, axis=0)


def grouped(
    groups, adj, src, own_sum,
    stage, packed, own_f, fb, rem, out_code, in_code,
    load_sem, own_sem, fsend, frecv, psend, precv,
):
    n_row, n_col = 4, 8
    r, c = lax.axis_index("row"), lax.axis_index("col")
    dst, width = adj.shape
    depth, roots = src.shape
    part = dst // n_row
    wide = width // n_col * 4
    lanes = width // 4
    tile = dst // 2
    scale = LEVELS / math.log(width * 64 * 1.01 / LOW)
    last = len(groups) - 1
    firsts = [sum(groups[:g]) for g in range(len(groups))]
    pair, east, north = flip(c, 1), flip(c, 2), flip(c, 4)
    diagonal = flip(east, 4)
    slots = [c, pair, east, north, flip(pair, 2), flip(pair, 4), diagonal, flip(diagonal, 1)]
    blocks = [0, 0, 1, 2, 1, 2, 3, 3]
    middle = jnp.logical_or(r == 1, r == 2)
    high = r // 2
    relay = 1 + high
    order = []
    for a, b in zip((3, 2, 1), (2, 3, 0)):
        low = jnp.where(middle, b, a)
        order.append(low + high * (3 - 2 * low))
    senders = [
        jnp.where(middle, 2 - high, 1 + high),
        jnp.where(middle, 3 - 3 * high, 2 - high),
    ]

    def chosen(step, values):
        value = values[0]
        for number in range(1, len(values)):
            value = jnp.where(step == number, values[number], value)
        return value

    barrier = pltpu.get_barrier_semaphore()
    for mate in (pair, east, north):
        pl.semaphore_signal(barrier, inc=1, device_id={"col": mate}, device_id_type=MESH)
    for other in senders:
        pl.semaphore_signal(barrier, inc=1, device_id={"row": other}, device_id_type=MESH)

    @pl.when(middle)
    def _():
        pl.semaphore_signal(barrier, inc=1, device_id={"row": 3 * high}, device_id_type=MESH)

    frontier_copy = pltpu.make_async_copy(src, own_f, own_sem)
    frontier_copy.start()

    def load(b, i):
        lane = pl.multiple_of(chosen(b, [slots[k] // 2 * lanes for k in (0, 2, 3, 6)]), lanes)
        lines = pl.ds(pl.multiple_of(i * tile, tile), tile)
        return pltpu.make_async_copy(
            adj.at[lines, pl.ds(lane, lanes)], stage.at[b, lines], load_sem.at[b, i]
        )

    for b in (0, 1):
        load(b, 0).start()
        load(b, 1).start()

    line = lax.broadcasted_iota(jnp.int32, (256, 256), 0)
    place = lax.broadcasted_iota(jnp.int32, (256, 256), 1)
    target = (line % 8) * 32 + ((line // 8) % 4) * 8 + line // 32
    shuffle = jnp.where(target == place, 1.0, 0.0).astype(jnp.bfloat16)
    frontier_copy.wait()
    for block in range(depth // 256):
        columns = slice(block * 256, block * 256 + 256)
        fb[c, :, columns] = lax.dot_general(
            own_f[columns, :], shuffle, (((0,), (0,)), ((), ())), preferred_element_type=jnp.float32
        ).astype(jnp.bfloat16)

    def rows(g):
        return pl.ds(firsts[g], groups[g])

    def send(ref, g, role, i, mate):
        number = g * ROLES + (0, 1, 5, 9, 9, 13, 15, 17)[role] + i
        return pltpu.make_async_remote_copy(
            src_ref=ref, dst_ref=ref, send_sem=fsend.at[number], recv_sem=frecv.at[number],
            device_id={"col": mate}, device_id_type=MESH,
        )

    def piece(g, role, i, slot):
        size = depth // 4 if role < 5 else depth // 2
        return fb.at[slot, rows(g), pl.ds(i * size, size)]

    def to_pair(g):
        return send(fb.at[c, rows(g)], g, 0, 0, pair)

    def message(g, role, i):
        source, mate = {
            1: (c, east), 2: (c, north), 3: (east, north), 4: (north, east),
            5: (east, pair), 6: (north, pair), 7: (diagonal, pair),
        }[role]
        return send(piece(g, role, i, source), g, role, i, mate)

    def arrived(g, role, i):
        slot = {1: 2, 2: 3, 3: 6, 4: 6, 5: 4, 6: 5, 7: 7}[role]
        send(piece(g, role, i, slots[slot]), g, role, i, pair).wait_recv()

    def first_sends(g):
        for i in range(4):
            message(g, 1, i).start()
            message(g, 2, (i + 2) % 4).start()

    def forward(g, i):
        arrived(g, 1, i)
        message(g, 3, i).start()
        arrived(g, 2, i + 2)
        message(g, 4, i + 2).start()

    def forward_rest(g):
        forward(g, 1)
        if g < last:
            first_sends(g + 1)
        message(g, 5, 0).start()
        message(g, 6, 1).start()

    def share_rest(g):
        arrived(g, 1, 2)
        arrived(g, 1, 3)
        message(g, 5, 1).start()
        arrived(g, 2, 0)
        arrived(g, 2, 1)
        message(g, 6, 0).start()

    def share_diagonal(g):
        arrived(g, 3, 0)
        arrived(g, 3, 1)
        message(g, 7, 0).start()
        arrived(g, 4, 2)
        arrived(g, 4, 3)
        message(g, 7, 1).start()

    pl.semaphore_wait(barrier, 5 + jnp.where(middle, 1, 0))
    first_sends(0)
    for g in range(len(groups)):
        to_pair(g).start()
    for b in (2, 3):
        load(b, 0).start()
        load(b, 1).start()

    def turn(b, i):
        load(b, i).wait()
        columns = pl.ds(pl.multiple_of(i * tile, tile), tile)
        turned = stage[b, columns, :].T.reshape(lanes // 8, 8, tile)
        spread = jnp.concatenate([turned, turned >> 8, turned >> 16, turned >> 24], axis=1)
        target = pl.ds(pl.multiple_of(b * lanes * 4, lanes * 4), lanes * 4)
        packed[target, columns] = spread.reshape(lanes * 4, tile).astype(jnp.int8)

    def product(lhs, slot, block, start, size):
        base = pl.multiple_of(block * lanes * 4 + lax.rem(slot, 2) * wide, wide)
        return lax.dot_general(
            lhs, unpack(packed[pl.ds(base, wide), pl.ds(start, size)]), (((1,), (0,)), ((), ())),
            preferred_element_type=jnp.float32,
        )

    def add_step(span, pairs):
        for t in range(3):
            start = pl.multiple_of(order[t] * part, part)
            value = rem[t, span, :]
            for slot, block in pairs:
                value = value + product(fb[slot, span, :], slot, block, start, part)
            rem[t, span, :] = value

    def exchange(g, t, slot, other):
        return pltpu.make_async_remote_copy(
            src_ref=out_code.at[t, rows(g)], dst_ref=in_code.at[slot, rows(g)], send_sem=psend.at[g, t],
            recv_sem=precv.at[g, slot], device_id={"row": other}, device_id_type=MESH,
        )

    def received(g, slot):
        exchange(g, 0, slot, relay).wait_recv()
        return decode(in_code[slot, rows(g), :], scale)

    def pass_on(g):
        @pl.when(middle)
        def _():
            out_code[1, rows(g), :] = encode(rem[1, rows(g), :] + received(g, n_row), scale)
            exchange(g, 1, r, order[1]).start()

    rem[...] = jnp.zeros_like(rem)

    @pl.loop(0, 2)
    def _(i):
        turn(0, i)

    @pl.loop(0, 2)
    def _(step):
        @pl.when(step == 1)
        def _():
            forward(0, 0)
            for g in range(len(groups)):
                send(fb.at[pair, rows(g)], g, 0, 0, pair).wait_recv()

        add_step(pl.ds(0, roots), [(chosen(step, (c, pair)), 0)])
        for k in range(3):
            number = step * 3 + k
            turn(1 + number // 2, lax.rem(number, 2))

    forward_rest(0)

    for g in range(len(groups)):
        share_rest(g)

        @pl.loop(0, 2)
        def _(step):
            @pl.when(step == 1)
            def _():
                share_diagonal(g)
                if 0 < g < last:
                    forward(g + 1, 0)
                for i in (0, 1):
                    arrived(g, 5, i)
                    arrived(g, 6, i)

            add_step(rows(g), [(chosen(step, slots[k : k + 3 : 2]), k - 1) for k in (2, 3)])

        if g == 0 < last:
            forward(1, 0)
        if g:
            pass_on(g - 1)
        if g < last:
            forward_rest(g + 1)
        arrived(g, 7, 0)
        arrived(g, 7, 1)

        @pl.loop(0, 3)
        def _(t):
            target = chosen(t, order)
            start = pl.multiple_of(target * part, part)
            value = rem[t, rows(g), :]
            for slot in slots[6:]:
                value = value + product(fb[slot, rows(g), :], slot, 3, start, part)
            direct = jnp.logical_or(t != 1, jnp.logical_not(middle))

            @pl.when(direct)
            def _():
                out_code[t, rows(g), :] = encode(value, scale)
                first_edge = jnp.logical_and(t == 0, jnp.logical_not(middle))
                exchange(g, t, jnp.where(first_edge, n_row, r), jnp.where(first_edge, relay, target)).start()

            @pl.when(jnp.logical_not(direct))
            def _():
                rem[t, rows(g), :] = value

    quarter = part // 4

    @pl.loop(0, 4)
    def _(q):
        @pl.when(q == 2)
        def _():
            pass_on(last)

        start = pl.multiple_of(r * part + q * quarter, quarter)
        value = jnp.zeros((roots, quarter), jnp.float32)
        for slot, block in zip(slots, blocks):
            value = value + product(fb[slot], slot, block, start, quarter)
        own_sum[:, pl.ds(pl.multiple_of(q * quarter, quarter), quarter)] = value

    for g in range(len(groups)):
        to_pair(g).wait_send()
        for role, places in ((1, 4), (2, 4), (3, 2), (4, 2), (5, 2), (6, 2), (7, 2)):
            for i in range(places):
                message(g, role, i + 2 if role == 4 else i).wait_send()
    for g in range(last):
        for t in range(3):
            exchange(g, t, r, relay).wait_send()
    for g in range(len(groups)):
        for sender in senders:
            own_sum[rows(g), :] += received(g, sender)

        @pl.when(middle)
        def _():
            own_sum[rows(g), :] += received(g, 3 * high)

    for t in range(3):
        exchange(last, t, r, relay).wait_send()


def deliver(reached, visited, counts, bits, held, marked, sem):
    part, roots = held.shape
    size = part // 4

    def copy(i):
        span = pl.ds(i * size, size)
        return pltpu.make_async_copy(held.at[span, :], counts.at[span, :], sem.at[i])

    place = lax.broadcasted_iota(jnp.int32, (32, size), 0)
    for i in range(4):
        span = slice(i * size, i * size + size)
        kept, added = [], []
        for word in range(visited.shape[0]):
            value = reached[word * 32 : word * 32 + 32, span]
            unseen = ((visited[word : word + 1, span] >> place) & 1) == 0
            kept.append(jnp.where(unseen, value, 0.0))
            marks = jnp.where(jnp.logical_and(unseen, value > 0), jnp.int32(1) << place, 0)
            added.append(jnp.sum(marks, axis=0, keepdims=True))
        held[span, :] = jnp.concatenate(kept, axis=0).T
        marked[:, span] = visited[:, span] | jnp.concatenate(added, axis=0)
        if i:
            copy(i - 1).start()
    last = pltpu.make_async_copy(marked, bits, sem.at[4])
    copy(3).start()
    last.start()
    for i in range(4):
        copy(i).wait()
    last.wait()


def grouped_shards(adjacency, frontier, visited):
    dst, width = adjacency.shape
    depth, roots = frontier.shape
    part = dst // 4
    groups = (roots // 2, roots // 2)
    n_group = len(groups)
    anywhere = pl.BlockSpec(memory_space=pl.ANY)
    vmem = pl.BlockSpec(memory_space=pltpu.VMEM)
    dma = pltpu.SemaphoreType.DMA
    reached = pl.pallas_call(
        functools.partial(grouped, groups),
        out_shape=jax.ShapeDtypeStruct((roots, part), jnp.float32),
        in_specs=[anywhere] * 2,
        out_specs=vmem,
        scratch_shapes=[
            pltpu.VMEM((4, dst, width // 4), jnp.int32),
            pltpu.VMEM((width * 4, dst), jnp.int8),
            pltpu.VMEM((depth, roots), jnp.bfloat16),
            pltpu.VMEM((8, roots, depth), jnp.bfloat16),
            pltpu.VMEM((3, roots, part), jnp.float32),
            pltpu.VMEM((3, roots, part), jnp.int16),
            pltpu.VMEM((5, roots, part), jnp.int16),
            dma((4, 2)),
            dma,
            dma((n_group * ROLES,)),
            dma((n_group * ROLES,)),
            dma((n_group, 3)),
            dma((n_group, 5)),
        ],
        compiler_params=pltpu.CompilerParams(
            collective_id=0, has_side_effects=True, vmem_limit_bytes=53 * 2**20
        ),
    )(adjacency, frontier)
    return pl.pallas_call(
        deliver,
        out_shape=(
            jax.ShapeDtypeStruct((part, roots), jnp.float32),
            jax.ShapeDtypeStruct((visited.shape[0], part), jnp.int32),
        ),
        in_specs=[vmem] * 2,
        out_specs=(anywhere, anywhere),
        scratch_shapes=[
            pltpu.VMEM((part, roots), jnp.float32),
            pltpu.VMEM((visited.shape[0], part), jnp.int32),
            dma((5,)),
        ],
        compiler_params=pltpu.CompilerParams(vmem_limit_bytes=4 * 2**20),
    )(reached, visited)


def shards(n_row, n_col, adjacency, frontier, visited):
    dst, width = adjacency.shape
    depth, roots = frontier.shape
    part = dst // n_row
    tile = math.gcd(dst, 256)
    ft = jnp.transpose(frontier.reshape(depth // 32, 32, roots), (2, 1, 0)).reshape(roots, depth)
    vmem = pl.BlockSpec(memory_space=pltpu.VMEM)
    roles = 8 if n_col == 8 else n_col - 1
    dma = pltpu.SemaphoreType.DMA
    return pl.pallas_call(
        functools.partial(kernel, n_row, n_col),
        out_shape=(
            jax.ShapeDtypeStruct((part, roots), jnp.float32),
            jax.ShapeDtypeStruct((visited.shape[0], part), jnp.int32),
        ),
        in_specs=[pl.BlockSpec(memory_space=pl.ANY), vmem, vmem],
        out_specs=(vmem, vmem),
        scratch_shapes=[
            pltpu.VMEM((2, tile, width), jnp.int32),
            pltpu.VMEM((width, dst), jnp.int32),
            pltpu.VMEM((n_col, roots, depth), jnp.bfloat16),
            pltpu.VMEM((roots, dst), jnp.float32),
            pltpu.VMEM((n_row - 1, roots, part), jnp.int16),
            pltpu.VMEM((n_row - 1, roots, part), jnp.int16),
            dma((2,)),
            dma,
            dma((roles,)),
            dma((roles,)),
            dma((n_row - 1,)),
            dma((n_row - 1,)),
        ],
        compiler_params=pltpu.CompilerParams(
            collective_id=0, has_side_effects=True, vmem_limit_bytes=56 * 2**20
        ),
    )(adjacency, ft, visited)


def solution(mesh):
    placed = (P("col", "row"), P(("row", "col"), None), P(None, ("col", "row")))
    n_row, n_col = mesh.shape["row"], mesh.shape["col"]
    body = grouped_shards if (n_row, n_col) == (4, 8) else functools.partial(shards, n_row, n_col)
    return jax.shard_map(
        body,
        mesh=mesh,
        in_specs=placed,
        out_specs=(P(("col", "row"), None), P(None, ("col", "row"))),
        check_vma=False,
    )
```

profile of v0, /device:TPU:0, one launch (start us, length us, event | category | flops | bytes accessed | tf_op | source)
XLA Modules:
  0.0 42.7 jit_solution(9406758757462464940)
XLA Ops:
  0.6 0.0 copy-start
  0.6 41.1 %shard_map.50.reached = f32[128,1024]{1,0:T(8,128)S(1)} custom-call(s32[4096,512]{1,0:T(8,128)} %adj.1, bf16[2048,128]{1,0:T(8,128)(2,1)} %src.1), custom_call_target="tpu_custom_call" | custom-call | tf_op jit(solution)/shard_map/pallas_call | solution.py:573
  41.7 0.0 copy-done
  41.7 1.0 %shard_map.51 = (f32[1024,128]{1,0:T(8,128)}, s32[4,1024]{1,0:T(4,128)}) custom-call(f32[128,1024]{1,0:T(8,128)S(1)} %shard_map.50.reached, s32[4,1024]{1,0:T(4,128)S(1)} %copy-done), custom_call_target="tpu_custom_call" | custom-call | tf_op jit(solution)/shard_map/pallas_call | solution.py:597
Async XLA Ops:
  0.6 41.1 %copy-start = (s32[4,1024]{1,0:T(4,128)S(1)}, s32[4,1024]{1,0:T(4,128)}, u32[]{:S(2)}) copy-start(s32[4,1024]{1,0:T(4,128)} %visited.1) | copy-start | bytes 49156
where the time goes:
time: 42.8 us; the launch traced here: 42.7 us
  Pallas kernels  42 us (98%)
  between operations  0.65 us (2%)
    pallas_call x1, Pallas kernels, grouped_shards(): pl.pallas_call(functools.partial(grouped, groups), out_shape=jax.ShapeDty...  41.1 us
    pallas_call x1, Pallas kernels, grouped_shards(): pl.pallas_call(deliver, out_shape=(jax.ShapeDtypeStruct((part, roots), jn...  0.98 us

commit v1 on v0

--- a/solution.py
+++ b/solution.py
@@ -252,7 +252,7 @@
 
 def grouped(
     groups, adj, src, own_sum,
-    stage, packed, own_f, fb, rem, out_code, in_code,
+    stage, packed_own, packed, own_f, fb, rem, out_code, in_code,
     load_sem, own_sem, fsend, frecv, psend, precv,
 ):
     n_row, n_col = 4, 8
@@ -393,18 +393,18 @@
         load(b, 0).start()
         load(b, 1).start()
 
-    def turn(b, i):
-        load(b, i).wait()
+    def turn(out, b, i):
         columns = pl.ds(pl.multiple_of(i * tile, tile), tile)
         turned = stage[b, columns, :].T.reshape(lanes // 8, 8, tile)
         spread = jnp.concatenate([turned, turned >> 8, turned >> 16, turned >> 24], axis=1)
-        target = pl.ds(pl.multiple_of(b * lanes * 4, lanes * 4), lanes * 4)
-        packed[target, columns] = spread.reshape(lanes * 4, tile).astype(jnp.int8)
+        target = pl.ds(pl.multiple_of((b - 1) * lanes * 4, lanes * 4), lanes * 4) if out is packed else slice(None)
+        out[target, columns] = spread.reshape(lanes * 4, tile).astype(jnp.int8)
 
     def product(lhs, slot, block, start, size):
-        base = pl.multiple_of(block * lanes * 4 + lax.rem(slot, 2) * wide, wide)
+        ref, first = (packed, block - 1) if block else (packed_own, 0)
+        base = pl.multiple_of(first * lanes * 4 + lax.rem(slot, 2) * wide, wide)
         return lax.dot_general(
-            lhs, unpack(packed[pl.ds(base, wide), pl.ds(start, size)]), (((1,), (0,)), ((), ())),
+            lhs, unpack(ref[pl.ds(base, wide), pl.ds(start, size)]), (((1,), (0,)), ((), ())),
             preferred_element_type=jnp.float32,
         )
 
@@ -436,7 +436,8 @@
 
     @pl.loop(0, 2)
     def _(i):
-        turn(0, i)
+        load(0, i).wait()
+        turn(packed_own, 0, i)
 
     @pl.loop(0, 2)
     def _(step):
@@ -446,10 +447,12 @@
             for g in range(len(groups)):
                 send(fb.at[pair, rows(g)], g, 0, 0, pair).wait_recv()
 
+        numbers = [step * 3 + k for k in range(3)]
+        for number in numbers:
+            load(1 + number // 2, lax.rem(number, 2)).wait()
         add_step(pl.ds(0, roots), [(chosen(step, (c, pair)), 0)])
-        for k in range(3):
-            number = step * 3 + k
-            turn(1 + number // 2, lax.rem(number, 2))
+        for number in numbers:
+            turn(packed, 1 + number // 2, lax.rem(number, 2))
 
     forward_rest(0)
 
@@ -565,7 +568,7 @@
     dst, width = adjacency.shape
     depth, roots = frontier.shape
     part = dst // 4
-    groups = (roots // 2, roots // 2)
+    groups = (3 * roots // 8, 3 * roots // 8, roots // 4)
     n_group = len(groups)
     anywhere = pl.BlockSpec(memory_space=pl.ANY)
     vmem = pl.BlockSpec(memory_space=pltpu.VMEM)
@@ -577,7 +580,8 @@
         out_specs=vmem,
         scratch_shapes=[
             pltpu.VMEM((4, dst, width // 4), jnp.int32),
-            pltpu.VMEM((width * 4, dst), jnp.int8),
+            pltpu.VMEM((width, dst), jnp.int8),
+            pltpu.VMEM((width * 3, dst), jnp.int8),
             pltpu.VMEM((depth, roots), jnp.bfloat16),
             pltpu.VMEM((8, roots, depth), jnp.bfloat16),
             pltpu.VMEM((3, roots, part), jnp.float32),

time: 42.8 us -> 41.7 us (0.974)
  Pallas kernels: 42 us -> 40.7 us
    pallas_call x1, Pallas kernels: 41.1 us -> 39.8 us  [grouped_shards(): pl.pallas_call(functools.partial(grouped, groups), out_shape=jax.ShapeDty...]
where the time goes in v1:
time: 41.7 us; the launch traced here: 41.5 us
  Pallas kernels  40.7 us (98%)
  between operations  0.81 us (2%)
    pallas_call x1, Pallas kernels, grouped_shards(): pl.pallas_call(functools.partial(grouped, groups), out_shape=jax.ShapeDty...  39.8 us
    pallas_call x1, Pallas kernels, grouped_shards(): pl.pallas_call(deliver, out_shape=(jax.ShapeDtypeStruct((part, roots), jn...  0.98 us

profile of v1, /device:TPU:0, one launch (start us, length us, event | category | flops | bytes accessed | tf_op | source)
XLA Modules:
  0.0 41.5 jit_solution(17220141852149523349)
XLA Ops:
  0.6 0.0 copy-start
  0.6 39.8 %shard_map.50.reached = f32[128,1024]{1,0:T(8,128)S(1)} custom-call(s32[4096,512]{1,0:T(8,128)} %adj.1, bf16[2048,128]{1,0:T(8,128)(2,1)} %src.1), custom_call_target="tpu_custom_call" | custom-call | tf_op jit(solution)/shard_map/pallas_call | solution.py:576
  40.4 0.0 copy-done
  40.4 1.0 %shard_map.51 = (f32[1024,128]{1,0:T(8,128)}, s32[4,1024]{1,0:T(4,128)}) custom-call(f32[128,1024]{1,0:T(8,128)S(1)} %shard_map.50.reached, s32[4,1024]{1,0:T(4,128)S(1)} %copy-done), custom_call_target="tpu_custom_call" | custom-call | tf_op jit(solution)/shard_map/pallas_call | solution.py:601
Async XLA Ops:
  0.6 39.8 %copy-start = (s32[4,1024]{1,0:T(4,128)S(1)}, s32[4,1024]{1,0:T(4,128)}, u32[]{:S(2)}) copy-start(s32[4,1024]{1,0:T(4,128)} %visited.1) | copy-start | bytes 49156

commit v2 on v1

--- a/solution.py
+++ b/solution.py
@@ -465,6 +465,7 @@
             def _():
                 share_diagonal(g)
                 if 0 < g < last:
+                    pass_on(g - 1)
                     forward(g + 1, 0)
                 for i in (0, 1):
                     arrived(g, 5, i)
@@ -474,7 +475,7 @@
 
         if g == 0 < last:
             forward(1, 0)
-        if g:
+        if g == last > 0:
             pass_on(g - 1)
         if g < last:
             forward_rest(g + 1)

time: 41.7 us -> 42.5 us (1.019)
  Pallas kernels: 40.7 us -> 41.6 us
    pallas_call x1, Pallas kernels: 39.8 us -> 40.6 us  [grouped_shards(): pl.pallas_call(functools.partial(grouped, groups), out_shape=jax.ShapeDty...]
where the time goes in v2:
time: 42.5 us; the launch traced here: 42.4 us
  Pallas kernels  41.6 us (98%)
  between operations  0.81 us (2%)
    pallas_call x1, Pallas kernels, grouped_shards(): pl.pallas_call(functools.partial(grouped, groups), out_shape=jax.ShapeDty...  40.6 us
    pallas_call x1, Pallas kernels, grouped_shards(): pl.pallas_call(deliver, out_shape=(jax.ShapeDtypeStruct((part, roots), jn...  0.98 us

profile of v2, /device:TPU:0, one launch (start us, length us, event | category | flops | bytes accessed | tf_op | source)
XLA Modules:
  0.0 42.4 jit_solution(11890008278020802611)
XLA Ops:
  0.6 0.0 copy-start
  0.6 40.6 %shard_map.50.reached = f32[128,1024]{1,0:T(8,128)S(1)} custom-call(s32[4096,512]{1,0:T(8,128)} %adj.1, bf16[2048,128]{1,0:T(8,128)(2,1)} %src.1), custom_call_target="tpu_custom_call" | custom-call | tf_op jit(solution)/shard_map/pallas_call | solution.py:577
  41.3 0.0 copy-done
  41.3 1.0 %shard_map.51 = (f32[1024,128]{1,0:T(8,128)}, s32[4,1024]{1,0:T(4,128)}) custom-call(f32[128,1024]{1,0:T(8,128)S(1)} %shard_map.50.reached, s32[4,1024]{1,0:T(4,128)S(1)} %copy-done), custom_call_target="tpu_custom_call" | custom-call | tf_op jit(solution)/shard_map/pallas_call | solution.py:602
Async XLA Ops:
  0.6 40.6 %copy-start = (s32[4,1024]{1,0:T(4,128)S(1)}, s32[4,1024]{1,0:T(4,128)}, u32[]{:S(2)}) copy-start(s32[4,1024]{1,0:T(4,128)} %visited.1) | copy-start | bytes 49156
